TPU v7x, 32 devices: a whole 2x2x4 slice. The times are simulated.
32 devices in a mesh: cls: 8 (over z, y), row: 4 (over x, core).
Axes of the slice: x: 2, y: 2, z: 4, core: 2. Of those that a mesh axis runs over, the one named last changes fastest.
Arguments:
- embeddings: float32 [1024, 1024], P('row'), may hold values from -6 to 6
- weights: float32 [1024, 81920], P(('cls', 'row')), may hold values from -4 to 4
- labels: int32 [1024], replicated, may hold values from 0 to 81919, as said below
Outputs:
- weight_update: float32 [1024, 81920], P(None, ('cls', 'row'))
- losses: float32 [2, 1024], replicated
Inputs may be any that keep to these rules, and one draw needn't show every extreme that they name: labels take at most 512 distinct values, at most one in each aligned run of 160 classes; rows may share a label.
All inputs are finite; a program needn't handle non-finite values.
Results may differ from a plain program's by a relative error of at most 0.012.
The roundings to bfloat16 on the way count: a program that leaves them out, or rounds other values in their place, can miss the bound.
Values may be sent and summed in bfloat16 or wider, within the bound.
No kernel may reach another device: no remote copies, remote signals or barrier semaphores. Data moves between devices by JAX's collectives and lax.ppermute only.
A program may use at most 128 MiB of HBM per device.

v0:
```python
import jax
import jax.numpy as jnp
from jax import lax
from jax.sharding import PartitionSpec as P

STEPS = 2
learn_rate = 2.0


def shards(embeddings, weights, labels):
    peer_count = lax.axis_size(("cls", "row"))
    examples = lax.all_gather(embeddings.astype(jnp.bfloat16), "row", axis=0, tiled=True)
    row_count = examples.shape[0]
    feature_rows = weights.shape[0]
    class_count = weights.shape[1] // peer_count
    model_width = feature_rows * peer_count
    offset = lax.axis_index(("cls", "row")) * class_count
    columns = lax.broadcasted_iota(jnp.int32, (1, class_count), 1) + offset
    label_hit = columns == labels[:, None]
    pieces = weights.reshape(feature_rows, peer_count, class_count // 128, 128)
    block_weights = lax.all_to_all(pieces, ("cls", "row"), split_axis=1, concat_axis=0, tiled=True)[
        :, 0
    ]
    block_width = block_weights.shape[1] * 128
    flat_weights = block_weights.reshape(block_weights.shape[0], block_width)
    block_logits = jnp.dot(
        examples, flat_weights.astype(jnp.bfloat16), preferred_element_type=jnp.float32
    )
    first_logits = block_logits.reshape(row_count, block_weights.shape[1], 128)
    current = block_weights.reshape(model_width, class_count)
    logits = first_logits.reshape(row_count, class_count)
    starting = current
    loss_rows = []
    for step_index in range(STEPS):
        if step_index > 0:
            logits = jnp.dot(
                examples, current.astype(jnp.bfloat16), preferred_element_type=jnp.float32
            )
        local_peak = jnp.max(logits, axis=1)
        local_picked = jnp.sum(jnp.where(label_hit, logits, 0.0), axis=1)
        row_peak = lax.pmax(local_peak, ("cls", "row"))
        row_total, picked = lax.psum(
            (jnp.sum(jnp.exp(logits - row_peak[:, None]), axis=1), local_picked), ("cls", "row")
        )
        log_norm = row_peak + jnp.log(row_total)
        loss_rows.append(log_norm - picked)
        onehot = jnp.where(label_hit, 1.0, 0.0)
        residual = (jnp.exp(logits - log_norm[:, None]) - onehot).astype(jnp.bfloat16)
        gradient = (
            lax.dot_general(
                examples, residual, (((0,), (0,)), ((), ())), preferred_element_type=jnp.float32
            )
            / row_count
        )
        current = current - learn_rate * gradient
    return (current - starting, jnp.stack(loss_rows))


def solution(mesh):
    placed = (P("row", None), P(("cls", "row"), None), P())
    return jax.shard_map(
        shards,
        mesh=mesh,
        in_specs=placed,
        out_specs=(P(None, ("cls", "row")), P()),
        check_vma=False,
    )
```

profile of v0, /device:TPU:0, one launch (start us, length us, event | category | flops | bytes accessed | tf_op | source)
XLA Modules:
  0.0 578.8 jit_solution(8699041707677321800)
XLA Ops:
  7.2 9.4 %reshape.18 = f32[32,32,20,128]{3,2,1,0:T(8,128)} reshape(f32[32,81920]{1,0:T(8,128)} %param.4) | data formatting | bytes 20971520 | tf_op jit(solution)/shard_map/reshape | solution.py:20
  16.6 14.7 %copy.13 = f32[32,32,20,128]{3,0,2,1:T(8,128)} copy(f32[32,32,20,128]{3,2,1,0:T(8,128)} %reshape.18) | data formatting | bytes 20971520 | tf_op jit(solution)/shard_map/reshape | solution.py:20
  31.3 7.4 %all-to-all-start = ((f32[32,32,20,128]{3,0,2,1:T(8,128)}), f32[32,32,20,128]{3,0,2,1:T(8,128)}, u32[]{:S(2)}, u32[]{:S(2)}) async-start(f32[32,32,20,128]{3,0,2,1:T(8,128)} %copy.13), calls=%async_computation | async-start | bytes 20971520 | tf_op jit(solution)/shard_map/all_to_all | solution.py:21
  38.8 0.4 all-gather.2.cloned.1.call-start
  39.2 0.0 copy-done
  39.2 0.9 convert_element_type.15
  40.1 0.0 all-gather.2.cloned.1.call-update
  40.1 234.6 %all-to-all-done = f32[32,32,20,128]{3,0,2,1:T(8,128)} async-done(((f32[32,32,20,128]{3,0,2,1:T(8,128)}), f32[32,32,20,128]{3,0,2,1:T(8,128)}, u32[]{:S(2)}, u32[]{:S(2)}) %all-to-all-start) | async-done | bytes 10485792 | tf_op jit(solution)/shard_map/all_to_all | solution.py:21
  274.7 17.8 %copy.14 = f32[32,32,1,20,128]{4,3,1,0,2:T(8,128)} copy(f32[32,32,1,20,128]{4,1,3,0,2:T(8,128)} %bitcast.1) | data formatting | bytes 20971520 | tf_op jit(solution)/shard_map/all_to_all | solution.py:21
  292.5 21.9 %copy.21 = f32[128,8,20,128]{3,1,2,0:T(8,128)} copy(f32[128,8,20,128]{3,2,1,0:T(8,128)} %bitcast.41) | data formatting | bytes 20971520
  314.4 11.4 %copy.15 = f32[1024,2560]{0,1:T(8,128)} copy(f32[1024,2560]{1,0:T(8,128)} %bitcast.42) | data formatting | bytes 20971520 | tf_op jit(solution)/shard_map/reshape;squeeze | solution.py:30
  325.8 11.4 %fusion.35 = (f32[1024]{0:T(1024)S(1)}, f32[1024,2560]{1,0:T(8,128)}) fusion(bf16[1024,1024]{1,0:T(8,128)(2,1)} %all-gather.2.cloned.1.call-done, f32[1024,2560]{1,0:T(8,128)} %bitcast.43), kind=kOutput, calls=%fused_computation.45 | convolution fusion | flops 5373950976 | bytes 23072768 | tf_op jit(solution)/shard_map/dot_general | solution.py:26
  337.2 36.8 %pmax.14 = f32[1024]{0:T(1024)S(1)} all-reduce(f32[1024]{0:T(1024)S(1)} %get-tuple-element.17), channel_id=1, replica_groups=mesh['cls'=8,'row'=4] {'cls','row'}, use_global_device_ids=true, to_apply=%region_1.2 | all-reduce | flops 1024 | bytes 8192 | tf_op jit(solution)/shard_map/pmax | solution.py:41
  374.0 5.7 fusion.4
  379.7 41.0 %psum.28 = f32[1024]{0:T(1024)S(1)} all-reduce(f32[1024]{0:T(1024)S(1)} %get-tuple-element.9), channel_id=1, replica_groups=mesh['cls'=8,'row'=4] {'cls','row'}, use_global_device_ids=true, to_apply=%region_3.4 | all-reduce | flops 1024 | bytes 8192 | tf_op jit(solution)/shard_map/psum | solution.py:42
  420.7 12.0 %fusion.14 = f32[2560,1024]{1,0:T(8,128)} fusion(bf16[1024,1024]{1,0:T(8,128)(2,1)} %all-gather.2.cloned.1.call-done, f32[1024,2560]{1,0:T(8,128)} %get-tuple-element.18, s32[2560]{0:T(1024)S(1)} %iota_add_fusion, f32[1024]{0:T(1024)S(1)} %log_add_fusion.1, s32[1024]{0:T(1024)S(1)} %copy-done.1), kind=kOutput, calls=%fused_computation.21 | convolution fusion | flops 5381816320 | bytes 23087104 | tf_op jit(solution)/shard_map/dot_general | solution.py:50
  432.8 12.4 %fusion.36 = (f32[1024]{0:T(1024)S(1)}, f32[2560,1024]{1,0:T(8,128)}) fusion(bf16[1024,1024]{1,0:T(8,128)(2,1)S(1)} %copy-done.2, f32[1024,2560]{0,1:T(8,128)S(1)} %bitcast.45, f32[2560,1024]{1,0:T(8,128)} %fusion.14), kind=kOutput, calls=%fused_computation.46 | convolution fusion | flops 5379193856 | bytes 33558528 | tf_op jit(solution)/shard_map/dot_general | solution.py:36
  445.2 39.6 %pmax.15 = f32[1024]{0:T(1024)S(1)} all-reduce(f32[1024]{0:T(1024)S(1)} %get-tuple-element.19), channel_id=1, replica_groups=mesh['cls'=8,'row'=4] {'cls','row'}, use_global_device_ids=true, to_apply=%region_5.6 | all-reduce | flops 1024 | bytes 8192 | tf_op jit(solution)/shard_map/pmax | solution.py:41
  484.8 11.5 %copy.16 = f32[2560,1024]{0,1:T(8,128)} copy(f32[2560,1024]{1,0:T(8,128)} %get-tuple-element.20) | data formatting | bytes 20971520 | tf_op jit(solution)/shard_map/dot_general | solution.py:36
  496.3 5.6 fusion.5
  501.9 40.6 %all-reduce = (f32[1024]{0:T(1024)S(1)}, f32[1024]{0:T(1024)S(1)}, f32[1024]{0:T(1024)S(1)}) all-reduce(f32[1024]{0:T(1024)S(1)} %get-tuple-element.11, f32[1024]{0:T(1024)S(1)} %get-tuple-element.10, f32[1024]{0:T(1024)S(1)} %get-tuple-element.8), channel_id=1, replica_groups=mesh['cls'=8,'row'=4] {'cls','row'}, use_global_device_ids=true, to_apply=%region_7.8 | all-reduce | flops 3072 | bytes 24576 | tf_op jit(solution)/shard_map/psum | solution.py:42
  542.5 17.2 %fusion.6 = f32[1024,2560]{0,1:T(8,128)} fusion(f32[1024,2560]{0,1:T(8,128)} %copy.15, f32[2560,1024]{1,0:T(8,128)} %fusion.14, bf16[1024,1024]{1,0:T(8,128)(2,1)} %all-gather.2.cloned.1.call-done, f32[2560,1024]{0,1:T(8,128)} %copy.16, f32[1024]{0:T(1024)S(1)} %get-tuple-element.16, s32[2560]{0:T(1024)S(1)} %iota_add_fusion, s32[1024]{0:T(1024)S(1)} %copy-done.1), kind=kOutput, calls=%fused_computation.11 | convolution fusion | flops 5394923520 | bytes 44058624 | tf_op jit(solution)/shard_map/dot_general | solution.py:50
  559.7 11.4 %copy.18 = f32[1024,2560]{1,0:T(8,128)} copy(f32[1024,2560]{0,1:T(8,128)} %fusion.6) | data formatting | bytes 20971520
  571.1 0.6 pad_maximum_fusion
  (17 shorter events, 0.0 us)
Async XLA Ops:
  31.3 7.9 %copy-start = (f32[256,1024]{1,0:T(8,128)S(1)}, f32[256,1024]{1,0:T(8,128)}, u32[]{:S(2)}) copy-start(f32[256,1024]{1,0:T(8,128)} %param.3) | copy-start | bytes 3145732
  31.3 243.4 %all-to-all-start = ((f32[32,32,20,128]{3,0,2,1:T(8,128)}), f32[32,32,20,128]{3,0,2,1:T(8,128)}, u32[]{:S(2)}, u32[]{:S(2)}) async-start(f32[32,32,20,128]{3,0,2,1:T(8,128)} %copy.13), calls=%async_computation | async-start | bytes 20971520 | tf_op jit(solution)/shard_map/all_to_all | solution.py:21
  38.8 287.0 %all-gather.2.cloned.1.call-start = ((), (), s32[]{:S(2)}) async-start(), calls=%async_computation.1 | async-start | bytes 2621440 | tf_op jit(solution)/shard_map/all_gather | solution.py:12
  325.8 48.2 %copy-start.1 = (s32[1024]{0:T(1024)S(1)}, s32[1024]{0:T(1024)}, u32[]{:S(2)}) copy-start(s32[1024]{0:T(1024)} %param.5) | copy-start | bytes 12292
  374.0 58.8 %slice-start = ((s8[10485760]{0:T(1024)(128)(4,1)}), s8[2097152]{0:T(1024)(128)(4,1)S(1)}, s32[]{:S(2)}) async-start(s8[10485760]{0:T(1024)(128)(4,1)} %bitcast.44), calls=%async_computation.2 | async-start | bytes 4194304
  420.7 12.0 %slice-start.1 = ((s8[10485760]{0:T(1024)(128)(4,1)}), s8[4194304]{0:T(1024)(128)(4,1)S(1)}, s32[]{:S(2)}) async-start(s8[10485760]{0:T(1024)(128)(4,1)} %bitcast.44), calls=%async_computation.3 | async-start | bytes 8388608
  420.7 12.0 %slice-start.2 = ((s8[10485760]{0:T(1024)(128)(4,1)}), s8[4194304]{0:T(1024)(128)(4,1)S(1)}, s32[]{:S(2)}) async-start(s8[10485760]{0:T(1024)(128)(4,1)} %bitcast.44), calls=%async_computation.4 | async-start | bytes 8388608
  420.7 12.0 %copy-start.2 = (bf16[1024,1024]{1,0:T(8,128)(2,1)S(1)}, bf16[1024,1024]{1,0:T(8,128)(2,1)}, u32[]{:S(2)}) copy-start(bf16[1024,1024]{1,0:T(8,128)(2,1)} %all-gather.2.cloned.1.call-done) | copy-start | bytes 6291460
Sparse Core Ops, SparseCore 0:
  41.1 74.9 all-gather.1
where the time goes:
time: 585 us; the launch traced here: 579 us
  waiting for transfers between devices  235 us (40%)
  blocking collectives  158 us (27%)
  local copies, waits for them, and re-layouts  98.1 us (17%)
  matrix products  52.9 us (9%)
  between operations  14.3 us (2%)
  other arithmetic  12.8 us (2%)
  starting transfers between devices  7.86 us (1%)
    all_to_all x1, waiting for transfers between devices, shards(): lax.all_to_all(pieces, ('cls', 'row'), split_axis=1, concat_axis=0, tiled...  235 us
    psum x2, blocking collectives, shards(): lax.psum((jnp.sum(jnp.exp(logits - row_peak[:, None]), axis=1), local_pic...  81.7 us
    pmax x2, blocking collectives, shards(): row_peak = lax.pmax(local_peak, ('cls', 'row'))  76.4 us
    unnamed x14, local copies, waits for them, and re-layouts  33.3 us
    dot_general x2, matrix products, shards(): lax.dot_general(examples, residual, (((0,), (0,)), ((), ())), preferred_e...  29.2 us
    reshape x2, local copies, waits for them, and re-layouts, shards(): pieces = weights.reshape(feature_rows, peer_count, class_count // 128, 128)  24.2 us
    all_to_all x1, local copies, waits for them, and re-layouts, shards(): lax.all_to_all(pieces, ('cls', 'row'), split_axis=1, concat_axis=0, tiled...  17.8 us
    dot_general x1, matrix products, shards(): jnp.dot(examples, current.astype(jnp.bfloat16), preferred_element_type=jn...  12.4 us
  transfers between devices with their start and end apart: 2, of which 1 were waited for; matrix products, arithmetic and copies ran while one was open for 9% of the time, Pallas kernels for 0%

commit v1 on v0

--- a/solution.py
+++ b/solution.py
@@ -18,9 +18,15 @@
     columns = lax.broadcasted_iota(jnp.int32, (1, class_count), 1) + offset
     label_hit = columns == labels[:, None]
     pieces = weights.reshape(feature_rows, peer_count, class_count // 128, 128)
-    block_weights = lax.all_to_all(pieces, ("cls", "row"), split_axis=1, concat_axis=0, tiled=True)[
-        :, 0
-    ]
+    block_weights = jnp.concatenate(
+        lax.all_to_all(
+            jnp.stack(jnp.split(pieces, lax.axis_size(("cls", "row")), axis=1)),
+            ("cls", "row"),
+            0,
+            0,
+        ),
+        axis=0,
+    )[:, 0]
     block_width = block_weights.shape[1] * 128
     flat_weights = block_weights.reshape(block_weights.shape[0], block_width)
     block_logits = jnp.dot(

time: 585 us -> 613 us (1.048)
  local copies, waits for them, and re-layouts: 98.1 us -> 129 us
    unnamed x14 -> x45, local copies, waits for them, and re-layouts: 33.3 us -> 77.9 us
    reshape x2 -> x1, local copies, waits for them, and re-layouts: 24.2 us -> 9.43 us  [shards(): pieces = weights.reshape(feature_rows, peer_count, class_count // 128, 128)]
    another operation x0 -> x2, local copies, waits for them, and re-layouts: none -> 12.3 us  [shards(): jnp.stack(jnp.split(pieces, lax.axis_size(('cls', 'row')), axis=1))]
    dot_general x1 -> x0, local copies, waits for them, and re-layouts: 11.5 us -> none  [shards(): jnp.dot(examples, current.astype(jnp.bfloat16), preferred_element_type=jn...]
  transfers between devices with their start and end apart: 2 -> 2, of which waited for: 1 -> 1; matrix products, arithmetic and copies ran while one was open for 9% -> 7% of each run, Pallas kernels for 0% -> 0%
where the time goes in v1:
time: 613 us; the launch traced here: 611 us
  waiting for transfers between devices  235 us (38%)
  blocking collectives  158 us (26%)
  local copies, waits for them, and re-layouts  129 us (21%)
  matrix products  54.1 us (9%)
  between operations  14.1 us (2%)
  other arithmetic  13.5 us (2%)
  starting transfers between devices  7.66 us (1%)
    all_to_all x1, waiting for transfers between devices, shards(): lax.all_to_all(jnp.stack(jnp.split(pieces, lax.axis_size(('cls', 'row')),...  235 us
    psum x2, blocking collectives, shards(): lax.psum((jnp.sum(jnp.exp(logits - row_peak[:, None]), axis=1), local_pic...  81.7 us
    unnamed x45, local copies, waits for them, and re-layouts  77.9 us
    pmax x2, blocking collectives, shards(): row_peak = lax.pmax(local_peak, ('cls', 'row'))  76.4 us
    dot_general x2, matrix products, shards(): lax.dot_general(examples, residual, (((0,), (0,)), ((), ())), preferred_e...  30.4 us
    all_to_all x1, local copies, waits for them, and re-layouts, shards(): lax.all_to_all(jnp.stack(jnp.split(pieces, lax.axis_size(('cls', 'row')),...  17.8 us
    dot_general x1, matrix products, shards(): jnp.dot(examples, current.astype(jnp.bfloat16), preferred_element_type=jn...  12.3 us
    another operation x2, local copies, waits for them, and re-layouts, shards(): jnp.stack(jnp.split(pieces, lax.axis_size(('cls', 'row')), axis=1))  12.3 us
  transfers between devices with their start and end apart: 2, of which 1 were waited for; matrix products, arithmetic and copies ran while one was open for 7% of the time, Pallas kernels for 0%

profile of v1, /device:TPU:0, one launch (start us, length us, event | category | flops | bytes accessed | tf_op | source)
XLA Modules:
  0.0 611.1 jit_solution(14898318579559688674)
XLA Ops:
  7.2 9.4 %reshape.17 = f32[32,32,20,128]{3,2,1,0:T(8,128)} reshape(f32[32,81920]{1,0:T(8,128)} %param.4) | data formatting | bytes 20971520 | tf_op jit(solution)/shard_map/reshape | solution.py:20
  16.6 1.8 fusion.63
  18.4 1.8 fusion.62
  20.2 1.8 fusion.61
  34.4 1.8 fusion.53
  57.5 1.8 fusion.40
  71.7 1.8 fusion.32
  73.5 10.5 %copy.103 = f32[32,32,1,20,128]{4,1,3,2,0:T(8,128)} copy(f32[32,32,1,20,128]{4,3,1,2,0:T(8,128)} %fusion.32) | data formatting | bytes 20971520 | tf_op jit(solution)/shard_map/stack | solution.py:23
  84.0 7.4 %all-to-all-start = ((f32[32,32,1,20,128]{4,1,3,2,0:T(8,128)}), f32[32,32,1,20,128]{4,1,3,2,0:T(8,128)}, u32[]{:S(2)}, u32[]{:S(2)}) async-start(f32[32,32,1,20,128]{4,1,3,2,0:T(8,128)} %copy.103), calls=%async_computation | async-start | bytes 20971520 | tf_op jit(solution)/shard_map/all_to_all | solution.py:22
  92.7 234.7 %all-to-all-done = f32[32,32,1,20,128]{4,1,3,2,0:T(8,128)} async-done(((f32[32,32,1,20,128]{4,1,3,2,0:T(8,128)}), f32[32,32,1,20,128]{4,1,3,2,0:T(8,128)}, u32[]{:S(2)}, u32[]{:S(2)}) %all-to-all-start) | async-done | bytes 10485792 | tf_op jit(solution)/shard_map/all_to_all | solution.py:22
  327.4 17.8 %copy.104 = f32[32,32,1,20,128]{4,3,1,0,2:T(8,128)} copy(f32[32,32,1,20,128]{4,1,3,2,0:T(8,128)} %all-to-all-done) | data formatting | bytes 20971520 | tf_op jit(solution)/shard_map/all_to_all | solution.py:22
  345.2 11.4 %copy.141 = f32[128,8,20,128]{3,1,2,0:T(8,128)} copy(f32[128,8,20,128]{3,2,1,0:T(8,128)} %bitcast.241) | data formatting | bytes 20971520
  356.6 11.4 %copy.105 = f32[1024,2560]{0,1:T(8,128)} copy(f32[1024,2560]{1,0:T(8,128)} %bitcast.242) | data formatting | bytes 20971520 | tf_op jit(solution)/shard_map/reshape;squeeze;reshape | solution.py:36
  368.0 11.3 %fusion.70 = (f32[1024]{0:T(1024)S(1)}, f32[2560,1024]{1,0:T(8,128)}) fusion(bf16[1024,1024]{1,0:T(8,128)(2,1)} %all-gather.2.cloned.1.call-done, f32[1024,2560]{1,0:T(8,128)} %bitcast.243), kind=kOutput, calls=%fused_computation.113 | convolution fusion | flops 5373950976 | bytes 23072768 | tf_op jit(solution)/shard_map/dot_general | solution.py:32
  379.3 36.8 %pmax.14 = f32[1024]{0:T(1024)S(1)} all-reduce(f32[1024]{0:T(1024)S(1)} %get-tuple-element.17), channel_id=1, replica_groups=mesh['cls'=8,'row'=4] {'cls','row'}, use_global_device_ids=true, to_apply=%region_1.2 | all-reduce | flops 1024 | bytes 8192 | tf_op jit(solution)/shard_map/pmax | solution.py:47
  416.1 6.0 fusion.4
  422.2 41.0 %psum.28 = f32[1024]{0:T(1024)S(1)} all-reduce(f32[1024]{0:T(1024)S(1)} %get-tuple-element.9), channel_id=1, replica_groups=mesh['cls'=8,'row'=4] {'cls','row'}, use_global_device_ids=true, to_apply=%region_3.4 | all-reduce | flops 1024 | bytes 8192 | tf_op jit(solution)/shard_map/psum | solution.py:48
  463.2 12.0 %fusion.17 = f32[2560,1024]{1,0:T(8,128)} fusion(bf16[1024,1024]{1,0:T(8,128)(2,1)} %all-gather.2.cloned.1.call-done, f32[2560,1024]{1,0:T(8,128)} %get-tuple-element.18, s32[1024]{0:T(1024)S(1)} %copy-done.1, f32[1024]{0:T(1024)S(1)} %log_add_fusion.1, s32[2560]{0:T(1024)S(1)} %iota_add_fusion), kind=kOutput, calls=%fused_computation.25 | convolution fusion | flops 5381816320 | bytes 23087104 | tf_op jit(solution)/shard_map/dot_general | solution.py:56
  475.2 12.3 %fusion.71 = (f32[1024]{0:T(1024)S(1)}, f32[2560,1024]{1,0:T(8,128)}) fusion(bf16[1024,1024]{1,0:T(8,128)(2,1)S(1)} %copy-done.2, f32[1024,2560]{0,1:T(8,128)S(1)} %bitcast.245, f32[2560,1024]{1,0:T(8,128)} %fusion.17), kind=kOutput, calls=%fused_computation.114 | convolution fusion | flops 5379193856 | bytes 33558528 | tf_op jit(solution)/shard_map/dot_general | solution.py:42
  487.6 39.6 %pmax.15 = f32[1024]{0:T(1024)S(1)} all-reduce(f32[1024]{0:T(1024)S(1)} %get-tuple-element.19), channel_id=1, replica_groups=mesh['cls'=8,'row'=4] {'cls','row'}, use_global_device_ids=true, to_apply=%region_5.6 | all-reduce | flops 1024 | bytes 8192 | tf_op jit(solution)/shard_map/pmax | solution.py:47
  527.2 5.9 fusion.5
  533.1 40.7 %all-reduce = (f32[1024]{0:T(1024)S(1)}, f32[1024]{0:T(1024)S(1)}, f32[1024]{0:T(1024)S(1)}) all-reduce(f32[1024]{0:T(1024)S(1)} %get-tuple-element.11, f32[1024]{0:T(1024)S(1)} %get-tuple-element.10, f32[1024]{0:T(1024)S(1)} %get-tuple-element.8), channel_id=1, replica_groups=mesh['cls'=8,'row'=4] {'cls','row'}, use_global_device_ids=true, to_apply=%region_7.8 | all-reduce | flops 3072 | bytes 24576 | tf_op jit(solution)/shard_map/psum | solution.py:48
  573.8 18.4 %fusion.6 = f32[1024,2560]{0,1:T(8,128)} fusion(f32[1024,2560]{0,1:T(8,128)} %copy.105, f32[2560,1024]{1,0:T(8,128)} %fusion.17, bf16[1024,1024]{1,0:T(8,128)(2,1)} %all-gather.2.cloned.1.call-done, f32[2560,1024]{1,0:T(8,128)} %get-tuple-element.20, f32[1024]{0:T(1024)S(1)} %get-tuple-element.16, s32[1024]{0:T(1024)S(1)} %copy-done.1, ...), kind=kOutput, calls=%fused_computation.11 | convolution fusion | flops 5394923520 | bytes 44058624 | tf_op jit(solution)/shard_map/dot_general | solution.py:56
  592.3 11.4 %copy.107 = f32[1024,2560]{1,0:T(8,128)} copy(f32[1024,2560]{0,1:T(8,128)} %fusion.6) | data formatting | bytes 20971520
  (48 shorter events, 47.9 us)
Async XLA Ops:
  84.0 7.7 %copy-start = (f32[256,1024]{1,0:T(8,128)S(1)}, f32[256,1024]{1,0:T(8,128)}, u32[]{:S(2)}) copy-start(f32[256,1024]{1,0:T(8,128)} %param.3) | copy-start | bytes 3145732
  84.0 243.4 %all-to-all-start = ((f32[32,32,1,20,128]{4,1,3,2,0:T(8,128)}), f32[32,32,1,20,128]{4,1,3,2,0:T(8,128)}, u32[]{:S(2)}, u32[]{:S(2)}) async-start(f32[32,32,1,20,128]{4,1,3,2,0:T(8,128)} %copy.103), calls=%async_computation | async-start | bytes 20971520 | tf_op jit(solution)/shard_map/all_to_all | solution.py:22
  91.5 276.5 %all-gather.2.cloned.1.call-start = ((), (), s32[]{:S(2)}) async-start(), calls=%async_computation.1 | async-start | bytes 2621440 | tf_op jit(solution)/shard_map/all_gather | solution.py:12
  368.0 48.1 %copy-start.1 = (s32[1024]{0:T(1024)S(1)}, s32[1024]{0:T(1024)}, u32[]{:S(2)}) copy-start(s32[1024]{0:T(1024)} %param.5) | copy-start | bytes 12292
  416.1 59.1 %slice-start = ((s8[10485760]{0:T(1024)(128)(4,1)}), s8[2097152]{0:T(1024)(128)(4,1)S(1)}, s32[]{:S(2)}) async-start(s8[10485760]{0:T(1024)(128)(4,1)} %bitcast.244), calls=%async_computation.2 | async-start | bytes 4194304
  463.2 12.0 %slice-start.1 = ((s8[10485760]{0:T(1024)(128)(4,1)}), s8[4194304]{0:T(1024)(128)(4,1)S(1)}, s32[]{:S(2)}) async-start(s8[10485760]{0:T(1024)(128)(4,1)} %bitcast.244), calls=%async_computation.3 | async-start | bytes 8388608
  463.2 12.0 %slice-start.2 = ((s8[10485760]{0:T(1024)(128)(4,1)}), s8[4194304]{0:T(1024)(128)(4,1)S(1)}, s32[]{:S(2)}) async-start(s8[10485760]{0:T(1024)(128)(4,1)} %bitcast.244), calls=%async_computation.4 | async-start | bytes 8388608
  463.2 12.0 %copy-start.2 = (bf16[1024,1024]{1,0:T(8,128)(2,1)S(1)}, bf16[1024,1024]{1,0:T(8,128)(2,1)}, u32[]{:S(2)}) copy-start(bf16[1024,1024]{1,0:T(8,128)(2,1)} %all-gather.2.cloned.1.call-done) | copy-start | bytes 6291460
Sparse Core Ops, SparseCore 0:
  93.9 74.9 all-gather.1
